TPU v7x, 128 devices: a whole 4x4x4 slice. The times are simulated.
128 devices in a mesh: seq: 8 (over x, core), tp: 16 (over y, z).
Axes of the slice: x: 4, y: 4, z: 4, core: 2. Of those that a mesh axis runs over, the one named last changes fastest.
Arguments:
- vit_input: bfloat16 [8192, 1280], P(('seq', 'tp')), may hold values from -6 to 6
- image_lengths: int32 [8, 2], P('seq'), may hold values from 1 to 192, 256 in all within a row
- positions: int32 [2048], replicated, may hold values from 0 to 2047, each once
- vit_ln_gain: float32 [1280], replicated, may hold values from 0.25 to 1.75
- w_qkv: bfloat16 [1280, 3, 1280], P(None, None, 'tp'), may hold values from -0.15625 to 0.15625
- w_proj: bfloat16 [1280, 1280], P('tp'), may hold values from -0.15625 to 0.15625
- merger_ln_gain: float32 [1280], replicated, may hold values from 0.25 to 1.75
- merger_w1: bfloat16 [5120, 5120], P(None, 'tp'), may hold values from -0.078125 to 0.078125
- merger_w2: bfloat16 [5120, 8192], P('tp'), may hold values from -0.36336105 to 0.36336105
- norm_gain: float32 [8192], P('seq'), may hold values from 0.25 to 1.75
- gate_up_weight: bfloat16 [8192, 2, 29568], P('seq', None, 'tp'), may hold values from -0.0625 to 0.0625
- down_weight: bfloat16 [29568, 8192], P('tp', 'seq'), may hold values from -0.125 to 0.125
Outputs:
- mixed: bfloat16 [2048, 8192], P('tp', 'seq')
Inputs may be any that keep to these rules, and one draw needn't show every extreme that they name: `image_lengths`: each row sums to 256. `positions`: a permutation: every slot once.
All inputs are finite; a program needn't handle non-finite values.
Results may differ from a plain program's by a relative error of at most 0.038.
Values may be sent and summed in bfloat16 or wider, within the bound.
A program may use at most 128 MiB of HBM per device.

v0:
```python
import jax
import jax.numpy as jnp
from jax import lax
from jax.sharding import Mesh
from jax.sharding import PartitionSpec as P

D = 8192
HD = 80
TP = ("tp_0", "tp_1")
SEQ_TP = ("seq", "tp_0", "tp_1")


def from_everyone(x, axis):
    copies = jnp.broadcast_to(x, (lax.axis_size(axis), *x.shape))
    return lax.all_to_all(copies, axis, split_axis=0, concat_axis=0, tiled=True)


def laid_out(tiles, dim):
    shape = list(tiles.shape[1:])
    shape[dim] *= tiles.shape[0]
    return jnp.moveaxis(tiles, 0, dim).reshape(shape)


def gathered_copies(x, axis, dim):
    tiles = from_everyone(x, axis)
    return laid_out(tiles, dim)


def cut_along(x, dim, devices):
    before, after = (x.shape[:dim], x.shape[dim + 1 :])
    return jnp.moveaxis(x.reshape(*before, devices, -1, *after), dim, 0)


def sum_at_owner(x, axis, dim):
    devices = lax.axis_size(axis)
    tiles = lax.all_to_all(cut_along(x, dim, devices), axis, 0, 0, tiled=True)
    return jnp.sum(tiles.astype(jnp.float32), axis=0)


def over_copies(x, axis):
    everything = from_everyone(x, axis)
    return jnp.sum(everything, axis=0)


def sum_by_axis(x, axes, dim):
    if not axes:
        return x
    nearer = lax.psum_scatter(x, axes[0], scatter_dimension=dim, tiled=True)
    return sum_by_axis(nearer, axes[1:], dim)


def layer_norm(values, gain):
    mean = jnp.mean(values, axis=-1, keepdims=True)
    centered = values - mean
    variance = jnp.mean(centered * centered, axis=-1, keepdims=True)
    return centered * lax.rsqrt(variance + 1e-06) * gain


def image_ids(lengths, count):
    image_ends = jnp.cumsum(lengths) * 4
    patch_index = jnp.arange(count, dtype=jnp.int32)
    return jnp.sum((patch_index[:, None] >= image_ends[None, :]).astype(jnp.int32), axis=1)


def attend(query, keys, values, image_index):
    scores = jnp.einsum("qhe,khe->hqk", query, keys, preferred_element_type=jnp.float32) * HD ** (
        -0.5
    )
    same_image = image_index[:, None] == image_index[None, :]
    scores = jnp.where(same_image[None], scores, -1e30)
    top = jnp.max(scores, axis=-1, keepdims=True)
    expo = jnp.exp(scores - top)
    weights = (expo / jnp.sum(expo, axis=-1, keepdims=True)).astype(jnp.bfloat16)
    output = jnp.einsum("hqk,khe->qhe", weights, values, preferred_element_type=jnp.float32)
    return output.astype(jnp.bfloat16)


def slot_sources(positions):
    count = positions.shape[0]
    return jnp.zeros((count,), jnp.int32).at[positions].set(jnp.arange(count, dtype=jnp.int32))


def local(
    vit_input,
    image_lengths,
    positions,
    vit_ln_gain,
    w_qkv,
    w_proj,
    merger_ln_gain,
    merger_w1,
    merger_w2,
    norm_gain,
    gate_up_weight,
    down_weight,
):
    tp_size = lax.axis_size(TP)
    seq_size = lax.axis_size("seq")
    own_patches = vit_input.shape[0]
    patch_width = vit_input.shape[1]
    head_cols = w_qkv.shape[2]
    local_heads = head_cols // HD
    normed_patches = layer_norm(vit_input.astype(jnp.float32), vit_ln_gain).astype(jnp.bfloat16)
    w_qkv_flat = w_qkv.reshape(patch_width, 3 * head_cols)
    projected = jnp.dot(
        gathered_copies(normed_patches, TP, 0), w_qkv_flat, preferred_element_type=jnp.float32
    ).astype(jnp.bfloat16)
    group_patches = projected.shape[0]
    projected = projected.reshape(group_patches, 3, local_heads, HD)
    image_index = image_ids(image_lengths[0], group_patches)
    attended = attend(projected[:, 0], projected[:, 1], projected[:, 2], image_index).reshape(
        group_patches, head_cols
    )
    picked = attended
    attn_sum = sum_at_owner(
        jnp.dot(picked, w_proj, preferred_element_type=jnp.float32).astype(jnp.bfloat16), TP, 0
    )
    vit_out = vit_input.astype(jnp.float32) + attn_sum
    own_tokens = own_patches // 4
    merged_in = (
        layer_norm(vit_out, merger_ln_gain)
        .astype(jnp.bfloat16)
        .reshape(own_tokens, 4 * patch_width)
    )
    expanded = jax.nn.gelu(
        jnp.dot(gathered_copies(merged_in, TP, 0), merger_w1, preferred_element_type=jnp.float32),
        approximate=False,
    ).astype(jnp.bfloat16)
    picked = expanded
    vis_rows = sum_at_owner(
        jnp.dot(picked, merger_w2, preferred_element_type=jnp.float32).astype(jnp.bfloat16), TP, 0
    ).astype(jnp.bfloat16)
    blocks = lax.all_to_all(vis_rows, "seq", split_axis=1, concat_axis=0, tiled=True)
    gathered = lax.all_gather(blocks, TP, axis=0, tiled=True)
    col_width = gathered.shape[1]
    all_tokens = (
        gathered.reshape(tp_size, seq_size, own_tokens, col_width)
        .transpose(1, 0, 2, 3)
        .reshape(tp_size * seq_size * own_tokens, col_width)
    )
    seq_rows = all_tokens.shape[0]
    seq_tokens = jnp.take(all_tokens, slot_sources(positions), axis=0)
    token_values = seq_tokens.astype(jnp.float32)
    row_squares = over_copies(jnp.sum(token_values * token_values, axis=1), "seq")
    inverse_rms = lax.rsqrt(row_squares / D + 1e-06)
    normed = (token_values * inverse_rms[:, None] * norm_gain).astype(jnp.bfloat16)
    slice_width = seq_tokens.shape[1]
    hidden_width = gate_up_weight.shape[2]
    weight_flat = gate_up_weight.reshape(slice_width, 2 * hidden_width)
    out_rows = seq_rows // tp_size
    picked = normed
    gate_up = lax.psum_scatter(
        jnp.dot(picked, weight_flat, preferred_element_type=jnp.float32).astype(jnp.bfloat16),
        "seq",
        scatter_dimension=0,
        tiled=True,
    ).astype(jnp.float32)
    hidden = (jax.nn.silu(gate_up[:, :hidden_width]) * gate_up[:, hidden_width:]).astype(
        jnp.bfloat16
    )
    terms = jnp.dot(
        lax.all_gather(hidden, "seq", axis=0, tiled=True),
        down_weight,
        preferred_element_type=jnp.float32,
    )
    down_sum = sum_by_axis(terms.astype(jnp.bfloat16), TP, 0).astype(jnp.float32)
    residual = lax.dynamic_slice_in_dim(token_values, lax.axis_index(TP) * out_rows, out_rows, 0)
    return (residual + down_sum).astype(jnp.bfloat16)


def solution(mesh):
    finer = Mesh(mesh.devices.reshape(mesh.shape["seq"], 4, 4), ("seq", "tp_0", "tp_1"))
    in_specs = (
        P(SEQ_TP, None),
        P("seq", None),
        P(),
        P(),
        P(None, None, TP),
        P(TP, None),
        P(),
        P(None, TP),
        P(TP, None),
        P("seq"),
        P("seq", None, TP),
        P(TP, "seq"),
    )
    out_specs = P(TP, "seq")
    return jax.shard_map(local, mesh=finer, in_specs=in_specs, out_specs=out_specs, check_vma=False)
```

profile of v0, /device:TPU:1, one launch (start us, length us, event | category | flops | bytes accessed | tf_op | source)
XLA Modules:
  0.0 554.3 jit_solution(18318716780304703547)
XLA Ops:
  6.5 1.2 convert_reduce_fusion.1
  7.7 1.1 fusion.11
  8.9 1.0 fusion.13
  9.9 1.8 broadcast_in_dim.26
  11.7 8.6 %all-to-all-start = ((bf16[16,64,1280]{2,1,0:T(8,128)(2,1)}), bf16[16,64,1280]{2,1,0:T(8,128)(2,1)}, u32[]{:S(2)}, u32[]{:S(2)}) async-start(bf16[16,64,1280]{2,1,0:T(8,128)(2,1)} %broadcast_in_dim.26), calls=%async_computation | async-start | bytes 5242880 | tf_op jit(solution)/shard_map/all_to_all | solution.py:15
  20.4 0.0 all-gather.3.cloned.1.call-start
  20.4 0.2 reduce-window.8
  20.6 0.1 fusion.57
  20.7 34.7 %all-to-all-done = bf16[16,64,1280]{2,1,0:T(8,128)(2,1)} async-done(((bf16[16,64,1280]{2,1,0:T(8,128)(2,1)}), bf16[16,64,1280]{2,1,0:T(8,128)(2,1)}, u32[]{:S(2)}, u32[]{:S(2)}) %all-to-all-start) | async-done | bytes 2621472 | tf_op jit(solution)/shard_map/all_to_all | solution.py:15
  55.4 2.7 convolution_convert_fusion.4
  58.1 0.9 fusion.4
  59.0 1.9 copy-done.3
  60.9 1.0 fusion.3
  61.9 6.0 %convolution_convert_fusion.2 = bf16[1024,1280]{1,0:T(8,128)(2,1)} fusion(bf16[80,1280]{1,0:T(8,128)(2,1)S(1)} %copy-done.6, f32[1024,1024]{0,1:T(8,128)} %copy-done.3, f32[1024]{0:T(1024)S(1)} %fusion.3, f32[1024]{0:T(1024)S(1)} %get-tuple-element.5, s32[1024]{0:T(1024)S(1)} %fusion.57, bf16[1024,3,1,80]{0,3,1,2:T(8,128)(2,1)} %bitcast.64), kind=kOutput, calls=%fused_computation.14 | convolution fusion | flops 385171456 | bytes 7200768 | tf_op jit(solution)/shard_map/dot_general | solution.py:116
  67.9 37.0 %all_to_all.45 = bf16[16,64,1280]{2,1,0:T(8,128)(2,1)S(1)} all-to-all(bf16[16,64,1280]{2,1,0:T(8,128)(2,1)} %bitcast.55), channel_id=1, replica_groups=mesh['seq'=8,'tp_0'=4,'tp_1'=4] {'tp_0','tp_1'}, dimensions={0} | all-to-all | bytes 5242880 | tf_op jit(solution)/shard_map/all_to_all | solution.py:36
  104.9 0.4 convert_reduce_fusion
  105.3 0.1 fusion.56
  105.5 0.2 multiply_reduce_fusion.1
  105.7 0.1 multiply_convert_fusion.2
  105.8 0.8 reshape.148
  106.6 1.2 broadcast_in_dim.47
  107.8 33.7 %all_to_all.46 = bf16[16,16,5120]{2,1,0:T(8,128)(2,1)} all-to-all(bf16[16,16,5120]{2,1,0:T(8,128)(2,1)S(1)} %broadcast_in_dim.47), channel_id=1, replica_groups=mesh['seq'=8,'tp_0'=4,'tp_1'=4] {'tp_0','tp_1'}, dimensions={0} | all-to-all | bytes 5242880 | tf_op jit(solution)/shard_map/all_to_all | solution.py:15
  141.5 10.9 %convolution_convert_fusion.1 = bf16[256,8192]{1,0:T(8,128)(2,1)} fusion(bf16[320,8192]{1,0:T(8,128)(2,1)} %param.20, bf16[256,5120]{1,0:T(8,128)(2,1)} %bitcast.56, bf16[5120,320]{0,1:T(8,128)(2,1)S(1)} %copy-done), kind=kOutput, calls=%fused_computation.3 | convolution fusion | flops 2188460032 | bytes 15335424 | tf_op jit(solution)/shard_map/dot_general | solution.py:131
  152.4 50.3 %all_to_all.47 = bf16[16,16,8192]{2,1,0:T(8,128)(2,1)} all-to-all(bf16[16,16,8192]{2,1,0:T(8,128)(2,1)} %bitcast.54), channel_id=1, replica_groups=mesh['seq'=8,'tp_0'=4,'tp_1'=4] {'tp_0','tp_1'}, dimensions={0} | all-to-all | bytes 8388608 | tf_op jit(solution)/shard_map/all_to_all | solution.py:36
  202.7 2.9 reduce_sum.100
  205.7 16.6 %all_to_all.48 = bf16[16,8,1024]{2,0,1:T(8,128)(2,1)} all-to-all(bf16[16,8,1024]{2,0,1:T(8,128)(2,1)S(1)} %bitcast.59), channel_id=1, replica_groups=mesh['seq'=8,'tp_0'=4,'tp_1'=4] {'seq'}, dimensions={1} | all-to-all | bytes 524288 | tf_op jit(solution)/shard_map/all_to_all | solution.py:133
  222.3 0.0 all-gather.3.cloned.1.call-update
  222.3 0.0 reduce-scatter.4.cloned.1.call-start
  222.4 8.0 %scatter_custom_fusion = s32[2048]{0:T(1024)S(1)} fusion(s32[2048]{0:T(1024)S(1)} %compare_select_fusion.1, s32[2048]{0:T(1024)S(1)} %iota.7, s32[]{:T(128)} %constant.45.clone.1), kind=kCustom, calls=%fused_computation.97 | custom fusion | bytes 8196 | tf_op jit(solution)/shard_map/scatter | solution.py:80
  230.5 39.6 %all-gather.3.cloned.1.call-done = bf16[2048,1024]{1,0:T(8,128)(2,1)} async-done(((bf16[128,1024]{1,0:T(8,128)(2,1)}), bf16[2048,1024]{1,0:T(8,128)(2,1)}) %all-gather.3.cloned.1.call-update) | async-done | bytes 4194320 | tf_op jit(solution)/shard_map/all_gather | solution.py:134
  270.1 5.0 copy.21
  275.1 13.7 %gather_fusion = bf16[2048,1024]{1,0:T(8,128)(2,1)} fusion(bf16[2048,1024]{1,0:T(8,128)(2,1)} %bitcast.52, s32[2048]{0:T(1024)S(1)} %fusion.58), kind=kCustom, calls=%fused_computation | custom fusion | bytes 8396800 | tf_op jit(solution)/shard_map/jit(_take)/gather | solution.py:142
  288.8 3.1 multiply_reduce_fusion
  291.9 9.7 %all_to_all.49 = f32[8,1,2048]{2,1,0:T(1,128)S(1)} all-to-all(f32[8,1,2048]{2,1,0:T(1,128)S(1)} %broadcast_in_dim.50), channel_id=1, replica_groups=mesh['seq'=8,'tp_0'=4,'tp_1'=4] {'seq'}, dimensions={0} | all-to-all | bytes 131072 | tf_op jit(solution)/shard_map/all_to_all | solution.py:15
  301.7 0.1 reduce_sum.102
  301.7 22.3 %convolution_convert_fusion = bf16[2048,3696]{0,1:T(8,128)(2,1)} fusion(bf16[1024,3696]{0,1:T(8,128)(2,1)} %bitcast.60, f32[1024]{0:T(1024)S(1)} %copy-done.7, f32[2048]{0:T(1024)S(1)} %add_rsqrt_fusion, bf16[2048,1024]{1,0:T(8,128)(2,1)} %gather_fusion, pred[2048]{0:T(1024)(128)(4,1)S(1)} %compare_and_fusion), kind=kOutput, calls=%fused_computation.2 | convolution fusion | flops 15520202752 | bytes 26916864 | tf_op jit(solution)/shard_map/dot_general | solution.py:153
  324.1 0.0 all-gather.5.cloned.1.call-start
  324.1 82.0 %reduce-scatter.4.cloned.1.call-done = bf16[256,3696]{0,1:T(8,128)(2,1)} async-done(((bf16[2048,3696]{0,1:T(8,128)(2,1)}), bf16[256,3696]{0,1:T(8,128)(2,1)}) %reduce-scatter.4.cloned.1.call-update) | async-done | bytes 1892368 | tf_op jit(solution)/shard_map/reduce_scatter | solution.py:152
  406.1 1.8 convert_element_type.83
  407.9 1.6 fusion.6
  409.5 0.0 reduce-scatter.6.cloned.1.call-start
  409.6 50.5 %all-gather.5.cloned.1.call-done = bf16[2048,1848]{0,1:T(8,128)(2,1)} async-done(((bf16[256,1848]{0,1:T(8,128)(2,1)}), bf16[2048,1848]{0,1:T(8,128)(2,1)}) %all-gather.5.cloned.1.call-update) | async-done | bytes 7569424 | tf_op jit(solution)/shard_map/all_gather | solution.py:162
  460.1 13.7 %convolution_convert_fusion.3 = bf16[2048,1024]{1,0:T(8,128)(2,1)} fusion(bf16[2048,1848]{0,1:T(8,128)(2,1)} %all-gather.5.cloned.1.call-done, bf16[1848,1024]{1,0:T(8,128)(2,1)} %param.23), kind=kOutput, calls=%fused_computation.15 | convolution fusion | flops 7753170944 | bytes 15548416 | tf_op jit(solution)/shard_map/dot_general | solution.py:161
  473.9 0.0 reduce-scatter.8.cloned.1.call-start
  473.9 47.4 %reduce-scatter.6.cloned.1.call-done = bf16[512,1024]{1,0:T(8,128)(2,1)} async-done(((bf16[2048,1024]{1,0:T(8,128)(2,1)}), bf16[512,1024]{1,0:T(8,128)(2,1)}) %reduce-scatter.6.cloned.1.call-update) | async-done | bytes 1048592 | tf_op jit(solution)/shard_map/reduce_scatter | solution.py:48
  521.4 5.3 fusion.95
  526.7 19.2 %reduce-scatter.8.cloned.1.call-done = bf16[128,1024]{1,0:T(8,128)(2,1)} async-done(((bf16[512,1024]{1,0:T(8,128)(2,1)}), bf16[128,1024]{1,0:T(8,128)(2,1)}) %reduce-scatter.8.cloned.1.call-update) | async-done | bytes 262160 | tf_op jit(solution)/shard_map/reduce_scatter | solution.py:48
  545.9 1.9 add_convert_fusion
  (35 shorter events, 0.2 us)
Async XLA Ops:
  6.5 134.9 %copy-start = (bf16[5120,320]{0,1:T(8,128)(2,1)S(1)}, bf16[5120,320]{0,1:T(8,128)(2,1)}, u32[]{:S(2)}) copy-start(bf16[5120,320]{0,1:T(8,128)(2,1)} %param.19) | copy-start | bytes 9830404
  8.9 11.5 %copy-start.8 = (s32[1,2]{1,0:T(1,128)S(1)}, s32[1,2]{1,0:T(1,128)}, u32[]{:S(2)}) copy-start(s32[1,2]{1,0:T(1,128)} %param.13) | copy-start | bytes 28
  11.7 43.6 %all-to-all-start = ((bf16[16,64,1280]{2,1,0:T(8,128)(2,1)}), bf16[16,64,1280]{2,1,0:T(8,128)(2,1)}, u32[]{:S(2)}, u32[]{:S(2)}) async-start(bf16[16,64,1280]{2,1,0:T(8,128)(2,1)} %broadcast_in_dim.26), calls=%async_computation | async-start | bytes 5242880 | tf_op jit(solution)/shard_map/all_to_all | solution.py:15
  20.4 249.7 %all-gather.3.cloned.1.call-start = ((), (), s32[]{:S(2)}) async-start(), calls=%async_computation.9 | async-start | bytes 4456448 | tf_op jit(solution)/shard_map/all_gather | solution.py:134
  58.1 0.9 copy-start.9
  58.1 3.8 copy-start.6
  59.0 1.9 copy-start.3
  67.9 37.4 %copy-start.2 = (bf16[64,1280]{1,0:T(8,128)(2,1)S(1)}, bf16[64,1280]{1,0:T(8,128)(2,1)}, u32[]{:S(2)}) copy-start(bf16[64,1280]{1,0:T(8,128)(2,1)} %param.12) | copy-start | bytes 491524
  67.9 37.7 %copy-start.5 = (f32[1280]{0:T(1024)S(1)}, f32[1280]{0:T(1024)}, u32[]{:S(2)}) copy-start(f32[1280]{0:T(1024)} %param.18) | copy-start | bytes 15364
  202.7 19.6 %copy-start.4 = (s32[2048]{0:T(1024)S(1)}, s32[2048]{0:T(1024)}, u32[]{:S(2)}) copy-start(s32[2048]{0:T(1024)} %param.14) | copy-start | bytes 24580
  222.3 183.8 %reduce-scatter.4.cloned.1.call-start = ((), (), s32[]{:S(2)}) async-start(), calls=%async_computation.10 | async-start | bytes 17031168 | tf_op jit(solution)/shard_map/reduce_scatter | solution.py:152
  288.8 13.0 %copy-start.7 = (f32[1024]{0:T(1024)S(1)}, f32[1024]{0:T(1024)}, u32[]{:S(2)}) copy-start(f32[1024]{0:T(1024)} %param.21) | copy-start | bytes 12292
  324.1 136.0 %all-gather.5.cloned.1.call-start = ((), (), s32[]{:S(2)}) async-start(), calls=%async_computation.11 | async-start | bytes 8515584 | tf_op jit(solution)/shard_map/all_gather | solution.py:162
  409.5 111.8 %reduce-scatter.6.cloned.1.call-start = ((), (), s32[]{:S(2)}) async-start(), calls=%async_computation.12 | async-start | bytes 5242880 | tf_op jit(solution)/shard_map/reduce_scatter | solution.py:48
  473.9 72.1 %reduce-scatter.8.cloned.1.call-start = ((), (), s32[]{:S(2)}) async-start(), calls=%async_computation.13 | async-start | bytes 1310720 | tf_op jit(solution)/shard_map/reduce_scatter | solution.py:48
  521.4 26.4 %copy-start.1 = (bf16[5120,320]{0,1:T(8,128)(2,1)S(1)}, bf16[5120,320]{0,1:T(8,128)(2,1)}, u32[]{:S(2)}) copy-start(bf16[5120,320]{0,1:T(8,128)(2,1)} %param.19) | copy-start | bytes 9830404
Sparse Core Ops, SparseCore 0:
  222.4 47.6 all-gather.2
  324.2 81.8 reduce-scatter.3
  409.6 50.4 all-gather.4
  474.0 47.3 reduce-scatter.5
  523.6 22.2 reduce-scatter.7
where the time goes:
time: 556 us; the launch traced here: 554 us
  waiting for transfers between devices  274 us (49%)
  blocking collectives  147 us (26%)
  matrix products  56.6 us (10%)
  local copies, waits for them, and re-layouts  32.5 us (6%)
  other arithmetic  22.1 us (4%)
  between operations  13.4 us (2%)
  starting transfers between devices  8.84 us (2%)
    all_to_all x2, blocking collectives, sum_at_owner(): tiles = lax.all_to_all(cut_along(x, dim, devices), axis, 0, 0, tiled=True)  87.3 us
    reduce_scatter x1, waiting for transfers between devices, local(): lax.psum_scatter(jnp.dot(picked, weight_flat, preferred_element_type=jnp....  82 us
    reduce_scatter x2, waiting for transfers between devices, sum_by_axis(): nearer = lax.psum_scatter(x, axes[0], scatter_dimension=dim, tiled=True)  66.6 us
    all_gather x1, waiting for transfers between devices, local(): lax.all_gather(hidden, 'seq', axis=0, tiled=True)  50.5 us
    all_to_all x2, blocking collectives, from_everyone(): return lax.all_to_all(copies, axis, split_axis=0, concat_axis=0, tiled=True)  43.4 us
    all_gather x1, waiting for transfers between devices, local(): gathered = lax.all_gather(blocks, TP, axis=0, tiled=True)  39.6 us
    all_to_all x1, waiting for transfers between devices, from_everyone(): return lax.all_to_all(copies, axis, split_axis=0, concat_axis=0, tiled=True)  34.7 us
    dot_general x1, matrix products, local(): jnp.dot(picked, weight_flat, preferred_element_type=jnp.float32)  22.3 us
  transfers between devices with their start and end apart: 6, of which 6 were waited for; matrix products, arithmetic and copies ran while one was open for 2% of the time, Pallas kernels for 0%

commit v1 on v0

--- a/solution.py
+++ b/solution.py
@@ -1,8 +1,280 @@
+import functools
 import jax
 import jax.numpy as jnp
 from jax import lax
+from jax.experimental import pallas as pl
+from jax.experimental.pallas import tpu as pltpu
 from jax.sharding import Mesh
 from jax.sharding import PartitionSpec as P
+
+MESH_ID = pl.DeviceIdType.MESH
+AXES = ("tp_0", "tp_1")
+
+
+def ring(axis, step):
+    return {axis: lax.rem(lax.axis_index(axis) + step, 4)}
+
+
+def remote(src, dst, send, recv, target):
+    return pltpu.make_async_remote_copy(
+        src_ref=src, dst_ref=dst, send_sem=send, recv_sem=recv, device_id=target, device_id_type=MESH_ID
+    )
+
+
+def greet(targets):
+    barrier = pltpu.get_barrier_semaphore()
+    for target in targets:
+        pl.semaphore_signal(barrier, inc=1, device_id=target, device_id_type=MESH_ID)
+    pl.semaphore_wait(barrier, len(targets))
+
+
+def plane_neighbours():
+    return [ring(axis, step) for axis in AXES for step in (1, 3)]
+
+
+def gather_plane(own, slot, half_cut, quarter_cut, send, recv, ready=None):
+    here = [lax.axis_index(axis) for axis in AXES]
+    sent = []
+
+    def place(half, first, second):
+        offsets = (first, second) if half == 0 else (second, first)
+        spots = [lax.rem(at + off, 4) for at, off in zip(here, offsets)]
+        return slot(spots[0] * 4 + spots[1])
+
+    def source(half, first, second):
+        return own if (first, second) == (0, 0) else place(half, first, second)
+
+    def start(half, phase, kind, axis, step, first, second, cut):
+        at = half * 20 + phase * 4 + kind
+        copy = remote(
+            cut(source(half, first, second)), cut(place(half, first, second)), send.at[at], recv.at[at], ring(axis, step)
+        )
+        copy.start()
+        sent.append(copy)
+
+    def landed(half, phase, kind, axis, first, second, cut):
+        at = half * 20 + phase * 4 + kind
+        target = cut(place(half, first, second))
+        remote(target, target, send.at[at], recv.at[at], ring(axis, 1)).wait_recv()
+
+    def axes(half):
+        return (AXES[0], AXES[1]) if half == 0 else (AXES[1], AXES[0])
+
+    def cuts(half):
+        return (
+            lambda ref: half_cut(ref, half),
+            lambda ref: quarter_cut(ref, 2 * half),
+            lambda ref: quarter_cut(ref, 2 * half + 1),
+        )
+
+    def spread(half, phase, first):
+        whole, _, _ = cuts(half)
+        axis = axes(half)[1]
+        start(half, phase, 0, axis, 1, first, 0, whole)
+        start(half, phase, 1, axis, 3, first, 0, whole)
+
+    def relay(half, phase, first):
+        whole, low, high = cuts(half)
+        axis = axes(half)[1]
+        landed(half, phase, 0, axis, first, 3, whole)
+        start(half, phase, 2, axis, 1, first, 3, low)
+        landed(half, phase, 1, axis, first, 1, whole)
+        start(half, phase, 3, axis, 3, first, 1, high)
+
+    def finish(half, phase, first):
+        whole, low, high = cuts(half)
+        axis = axes(half)[1]
+        landed(half, phase, 2, axis, first, 2, low)
+        landed(half, phase, 3, axis, first, 2, high)
+
+    for half in (0, 1):
+        whole, _, _ = cuts(half)
+        start(half, 0, 0, axes(half)[0], 1, 0, 0, whole)
+        start(half, 0, 1, axes(half)[0], 3, 0, 0, whole)
+    for half in (0, 1):
+        spread(half, 1, 0)
+    for half in (0, 1):
+        whole, low, high = cuts(half)
+        axis = axes(half)[0]
+        landed(half, 0, 0, axis, 3, 0, whole)
+        start(half, 0, 2, axis, 1, 3, 0, low)
+        spread(half, 2, 3)
+        landed(half, 0, 1, axis, 1, 0, whole)
+        start(half, 0, 3, axis, 3, 1, 0, high)
+        spread(half, 3, 1)
+    for half in (0, 1):
+        relay(half, 1, 0)
+    for half in (0, 1):
+        whole, low, high = cuts(half)
+        axis = axes(half)[0]
+        landed(half, 0, 2, axis, 2, 0, low)
+        landed(half, 0, 3, axis, 2, 0, high)
+        spread(half, 4, 2)
+    for phase, first in ((2, 3), (3, 1), (4, 2)):
+        for half in (0, 1):
+            relay(half, phase, first)
+    for phase, first in ((1, 0), (2, 3), (3, 1), (4, 2)):
+        for half in (0, 1):
+            finish(half, phase, first)
+    for copy in sent:
+        copy.wait_send()
+
+
+def reduce_plane(term, quarter_cut, got, made, sums, send, recv, emit):
+    here = [lax.axis_index(axis) for axis in AXES]
+    sent = []
+
+    def axes(half):
+        return (AXES[1], AXES[0]) if half == 0 else (AXES[0], AXES[1])
+
+    def part(half, first, second, which):
+        offsets = (first, second) if half == 0 else (second, first)
+        spots = [lax.rem(at + off, 4) for at, off in zip(here, offsets)]
+        return quarter_cut(term(spots[0] * 4 + spots[1]), 2 * half + which)
+
+    def phase_source(half, phase):
+        if phase < 4:
+            return lambda offset, which: part(half, phase, offset, which)
+        return lambda offset, which: sums.at[half * 8 + offset * 2 + which]
+
+    def slot(half, phase, kind):
+        return half * 30 + phase * 6 + kind
+
+    def start(half, phase, kind, src, step):
+        axis = axes(half)[0 if phase < 4 else 1]
+        at = slot(half, phase, kind)
+        copy = remote(src, got.at[at], send.at[at], recv.at[at], ring(axis, step))
+        copy.start()
+        sent.append(copy)
+
+    def landed(half, phase, kind):
+        at = slot(half, phase, kind)
+        axis = axes(half)[0 if phase < 4 else 1]
+        remote(got.at[at], got.at[at], send.at[at], recv.at[at], ring(axis, 1)).wait_recv()
+        return got[at].astype(jnp.float32)
+
+    def raw(half, phase):
+        own = phase_source(half, phase)
+        start(half, phase, 0, own(2, 0), 1)
+        start(half, phase, 3, own(2, 1), 3)
+        start(half, phase, 1, own(1, 1), 1)
+        start(half, phase, 4, own(3, 0), 3)
+
+    def summed(half, phase):
+        own = phase_source(half, phase)
+        for kind, offset, which, step in ((0, 1, 0, 1), (3, 3, 1, 3)):
+            at = half * 10 + phase * 2 + which
+            made[at] = (own(offset, which)[...].astype(jnp.float32) + landed(half, phase, kind)).astype(made.dtype)
+            start(half, phase, kind + 2, made.at[at], step)
+
+    def total(half, phase):
+        own = phase_source(half, phase)
+        return [
+            own(0, which)[...].astype(jnp.float32) + landed(half, phase, near) + landed(half, phase, far)
+            for which, near, far in ((0, 4, 2), (1, 1, 5))
+        ]
+
+    def settle(half, phase):
+        for which, value in enumerate(total(half, phase)):
+            sums[half * 8 + phase * 2 + which] = value.astype(sums.dtype)
+
+    order = (2, 1, 3, 0)
+    both = (0, 1)
+    for half in both:
+        raw(half, order[0])
+    for half in both:
+        raw(half, order[1])
+    for at, phase in enumerate(order):
+        for half in both:
+            summed(half, phase)
+        if at + 2 < 4:
+            for half in both:
+                raw(half, order[at + 2])
+        if at >= 1:
+            for half in both:
+                settle(half, order[at - 1])
+                if order[at - 1] == 2:
+                    own = phase_source(half, 4)
+                    start(half, 4, 0, own(2, 0), 1)
+                    start(half, 4, 3, own(2, 1), 3)
+                if order[at - 1] == 1:
+                    start(half, 4, 1, phase_source(half, 4)(1, 1), 1)
+                if order[at - 1] == 3:
+                    start(half, 4, 4, phase_source(half, 4)(3, 0), 3)
+    for half in both:
+        summed(half, 4)
+    for half in both:
+        settle(half, 0)
+    for half in both:
+        for which, value in enumerate(total(half, 4)):
+            emit(2 * half + which, value)
+    for copy in sent:
+        copy.wait_send()
+
+
+def cut_rows(ref, begin, size):
+    return ref.at[pl.ds(begin, size)]
+
+
+def plane_gather(block, collective_id, by_rows):
+    rows, cols = block.shape
+
+    def cutter(share):
+        def cut(ref, at):
+            if by_rows:
+                return ref.at[pl.ds(at * (rows // share), rows // share), :]
+            return ref.at[:, pl.ds(at * (cols // share), cols // share)]
+        return cut
+
+    def kernel(own, out, send, recv):
+        greet(plane_neighbours())
+        me = lax.axis_index("tp_0") * 4 + lax.axis_index("tp_1")
+        out[me] = own[...]
+        gather_plane(own, lambda t: out.at[t], cutter(2), cutter(4), send, recv)
+
+    return pl.pallas_call(
+        kernel,
+        out_shape=jax.ShapeDtypeStruct((16, rows, cols), block.dtype),
+        in_specs=[pl.BlockSpec(memory_space=pltpu.VMEM)],
+        out_specs=pl.BlockSpec(memory_space=pltpu.VMEM),
+        scratch_shapes=[pltpu.SemaphoreType.DMA((40,)), pltpu.SemaphoreType.DMA((40,))],
+        compiler_params=pltpu.CompilerParams(collective_id=collective_id, has_side_effects=True),
+        name=f"plane_gather_{collective_id}",
+    )(block)
+
+
+def plane_reduce(terms, collective_id, by_rows, out_dtype):
+    _, rows, cols = terms.shape
+    quarter = (rows // 4, cols) if by_rows else (rows, cols // 4)
+
+    def cut(ref, at):
+        if by_rows:
+            return ref.at[pl.ds(at * quarter[0], quarter[0]), :]
+        return ref.at[:, pl.ds(at * quarter[1], quarter[1])]
+
+    def kernel(terms_ref, out, got, made, sums, send, recv):
+        greet(plane_neighbours())
+
+        def emit(at, value):
+            cut(out, at)[...] = value.astype(out.dtype)
+
+        reduce_plane(lambda t: terms_ref.at[t], cut, got, made, sums, send, recv, emit)
+
+    return pl.pallas_call(
+        kernel,
+        out_shape=jax.ShapeDtypeStruct((rows, cols), out_dtype),
+        in_specs=[pl.BlockSpec(memory_space=pltpu.VMEM)],
+        out_specs=pl.BlockSpec(memory_space=pltpu.VMEM),
+        scratch_shapes=[
+            pltpu.VMEM((60, *quarter), terms.dtype),
+            pltpu.VMEM((20, *quarter), terms.dtype),
+            pltpu.VMEM((16, *quarter), terms.dtype),
+            pltpu.SemaphoreType.DMA((60,)),
+            pltpu.SemaphoreType.DMA((60,)),
+        ],
+        compiler_params=pltpu.CompilerParams(collective_id=collective_id, has_side_effects=True),
+        name=f"plane_reduce_{collective_id}",
+    )(terms)
 
 D = 8192
 HD = 80
@@ -103,7 +375,7 @@
     normed_patches = layer_norm(vit_input.astype(jnp.float32), vit_ln_gain).astype(jnp.bfloat16)
     w_qkv_flat = w_qkv.reshape(patch_width, 3 * head_cols)
     projected = jnp.dot(
-        gathered_copies(normed_patches, TP, 0), w_qkv_flat, preferred_element_type=jnp.float32
+        plane_gather(normed_patches, 1, True).reshape(-1, patch_width), w_qkv_flat, preferred_element_type=jnp.float32
     ).astype(jnp.bfloat16)
     group_patches = projected.shape[0]
     projected = projected.reshape(group_patches, 3, local_heads, HD)
@@ -112,9 +384,8 @@
         group_patches, head_cols
     )
     picked = attended
-    attn_sum = sum_at_owner(
-        jnp.dot(picked, w_proj, preferred_element_type=jnp.float32).astype(jnp.bfloat16), TP, 0
-    )
+    shares = jnp.dot(picked, w_proj, preferred_element_type=jnp.float32).astype(jnp.bfloat16)
+    attn_sum = plane_reduce(shares.reshape(tp_size, own_patches, patch_width), 2, True, jnp.float32)
     vit_out = vit_input.astype(jnp.float32) + attn_sum
     own_tokens = own_patches // 4
     merged_in = (
@@ -123,16 +394,15 @@
         .reshape(own_tokens, 4 * patch_width)
     )
     expanded = jax.nn.gelu(
-        jnp.dot(gathered_copies(merged_in, TP, 0), merger_w1, preferred_element_type=jnp.float32),
+        jnp.dot(plane_gather(merged_in, 3, False).reshape(-1, 4 * patch_width), merger_w1, preferred_element_type=jnp.float32),
         approximate=False,
     ).astype(jnp.bfloat16)
     picked = expanded
-    vis_rows = sum_at_owner(
-        jnp.dot(picked, merger_w2, preferred_element_type=jnp.float32).astype(jnp.bfloat16), TP, 0
-    ).astype(jnp.bfloat16)
+    shares = jnp.dot(picked, merger_w2, preferred_element_type=jnp.float32).astype(jnp.bfloat16)
+    vis_rows = plane_reduce(shares.reshape(tp_size, own_tokens, D), 4, False, jnp.bfloat16)
     blocks = lax.all_to_all(vis_rows, "seq", split_axis=1, concat_axis=0, tiled=True)
-    gathered = lax.all_gather(blocks, TP, axis=0, tiled=True)
-    col_width = gathered.shape[1]
+    gathered = plane_gather(blocks, 5, True)
+    col_width = gathered.shape[2]
     all_tokens = (
         gathered.reshape(tp_size, seq_size, own_tokens, col_width)
         .transpose(1, 0, 2, 3)

time: 556 us -> 466 us (0.84)
  blocking collectives: 147 us -> 10.2 us
  Pallas kernels: 0 us -> 113 us
  waiting for transfers between devices: 274 us -> 199 us
  starting transfers between devices: 8.84 us -> 15.5 us
    pallas_call x0 -> x5, Pallas kernels: none -> 113 us  [the longest x3 71.5 us: plane_gather(): pl.pallas_call(kernel, out_shape=jax.ShapeDtypeStruct((16, rows, cols), b...]
    all_to_all x3 -> x0, blocking collectives: 104 us -> none  [the longest x2 87.3 us: sum_at_owner(): tiles = lax.all_to_all(cut_along(x, dim, devices), axis, 0, 0, tiled=True)]
    all_gather x1 -> x0, waiting for transfers between devices: 39.6 us -> none  [local(): gathered = lax.all_gather(blocks, TP, axis=0, tiled=True)]
    all_to_all x1, waiting for transfers between devices: 34.7 us -> 0.01 us  [local(): lax.all_to_all(vis_rows, 'seq', split_axis=1, concat_axis=0, tiled=True)]
    all_to_all x2 -> x1, blocking collectives: 43.4 us -> 10.2 us  [from_everyone(): return lax.all_to_all(copies, axis, split_axis=0, concat_axis=0, tiled=True)]
    all_to_all x1, starting transfers between devices: 8.63 us -> 15.4 us  [local(): lax.all_to_all(vis_rows, 'seq', split_axis=1, concat_axis=0, tiled=True)]
  transfers between devices with their start and end apart: 6 -> 5, of which waited for: 6 -> 4; matrix products, arithmetic and copies ran while one was open for 2% -> 3% of each run, Pallas kernels for 0% -> 0%
where the time goes in v1:
time: 466 us; the launch traced here: 465 us
  waiting for transfers between devices  199 us (43%)
  Pallas kernels  113 us (24%)
  matrix products  56.7 us (12%)
  local copies, waits for them, and re-layouts  32.7 us (7%)
  other arithmetic  23.8 us (5%)
  starting transfers between devices  15.5 us (3%)
  between operations  13.4 us (3%)
  blocking collectives  10.2 us (2%)
    reduce_scatter x1, waiting for transfers between devices, local(): lax.psum_scatter(jnp.dot(picked, weight_flat, preferred_element_type=jnp....  81.9 us
    pallas_call x3, Pallas kernels, plane_gather(): pl.pallas_call(kernel, out_shape=jax.ShapeDtypeStruct((16, rows, cols), b...  71.5 us
    reduce_scatter x2, waiting for transfers between devices, sum_by_axis(): nearer = lax.psum_scatter(x, axes[0], scatter_dimension=dim, tiled=True)  66.6 us
    all_gather x1, waiting for transfers between devices, local(): lax.all_gather(hidden, 'seq', axis=0, tiled=True)  50.5 us
    pallas_call x2, Pallas kernels, plane_reduce(): pl.pallas_call(kernel, out_shape=jax.ShapeDtypeStruct((rows, cols), out_d...  41.6 us
    dot_general x1, matrix products, local(): jnp.dot(picked, weight_flat, preferred_element_type=jnp.float32)  22.3 us
    all_to_all x1, starting transfers between devices, local(): lax.all_to_all(vis_rows, 'seq', split_axis=1, concat_axis=0, tiled=True)  15.4 us
    dot_general x1, matrix products, local(): jnp.dot(lax.all_gather(hidden, 'seq', axis=0, tiled=True), down_weight, p...  13.7 us
  transfers between devices with their start and end apart: 5, of which 4 were waited for; matrix products, arithmetic and copies ran while one was open for 3% of the time, Pallas kernels for 0%

profile of v1, /device:TPU:1, one launch (start us, length us, event | category | flops | bytes accessed | tf_op | source)
XLA Modules:
  0.0 464.6 jit_solution(11867446840670153443)
XLA Ops:
  6.5 1.2 convert_reduce_fusion
  7.7 1.1 fusion.11
  8.9 1.7 fusion.13.own
  10.6 24.0 %plane_gather_1.1 = bf16[16,64,1280]{2,1,0:T(8,128)(2,1)} custom-call(bf16[64,1280]{1,0:T(8,128)(2,1)} %fusion.13.own), custom_call_target="tpu_custom_call" | custom-call | tf_op jit(solution)/shard_map/plane_gather_1/pallas_call | solution.py:235
  34.6 0.8 reduce-window.8
  35.4 0.1 fusion.57
  35.5 2.7 convolution_convert_fusion.4
  38.2 0.9 fusion.4
  39.1 1.9 copy-done.3
  41.0 1.0 fusion.3
  42.1 0.0 copy-start.2
  42.1 0.0 copy-start.6
  42.1 6.0 %convolution_convert_fusion.2 = bf16[1024,1280]{1,0:T(8,128)(2,1)} fusion(bf16[80,1280]{1,0:T(8,128)(2,1)} %param.17, f32[1024,1024]{0,1:T(8,128)} %copy-done.3, f32[1024]{0:T(1024)S(1)} %fusion.3, f32[1024]{0:T(1024)S(1)} %get-tuple-element.5, s32[1024]{0:T(1024)S(1)} %fusion.57, bf16[1024,3,1,80]{0,3,1,2:T(8,128)(2,1)} %bitcast.64), kind=kOutput, calls=%fused_computation.13 | convolution fusion | flops 385171456 | bytes 7200768 | tf_op jit(solution)/shard_map/dot_general | solution.py:387
  48.1 20.1 %plane_reduce_2.1 = f32[64,1280]{1,0:T(8,128)} custom-call(bf16[16,64,1280]{2,1,0:T(8,128)(2,1)} %bitcast.56), custom_call_target="tpu_custom_call" | custom-call | tf_op jit(solution)/shard_map/plane_reduce_2/pallas_call | solution.py:263
  68.2 1.1 fusion.56
  69.3 1.2 multiply_reduce_fusion.1
  70.5 1.8 multiply_convert_fusion.2
  72.3 1.7 reshape.148.own
  73.9 18.8 %plane_gather_3.1 = bf16[16,16,5120]{2,1,0:T(8,128)(2,1)} custom-call(bf16[16,5120]{1,0:T(8,128)(2,1)} %reshape.148.own), custom_call_target="tpu_custom_call" | custom-call | tf_op jit(solution)/shard_map/plane_gather_3/pallas_call | solution.py:235
  92.8 11.1 %convolution_convert_fusion.1 = bf16[256,8192]{1,0:T(8,128)(2,1)} fusion(bf16[320,8192]{1,0:T(8,128)(2,1)} %param.20, bf16[256,5120]{1,0:T(8,128)(2,1)} %bitcast.57, bf16[5120,320]{0,1:T(8,128)(2,1)S(1)} %copy-done), kind=kOutput, calls=%fused_computation.3 | convolution fusion | flops 2188460032 | bytes 15335424 | tf_op jit(solution)/shard_map/dot_general | solution.py:401
  103.9 21.5 %plane_reduce_4.1 = bf16[16,8192]{1,0:T(8,128)(2,1)} custom-call(bf16[16,16,8192]{2,1,0:T(8,128)(2,1)} %bitcast.54), custom_call_target="tpu_custom_call" | custom-call | tf_op jit(solution)/shard_map/plane_reduce_4/pallas_call | solution.py:263
  125.4 1.7 copy.23
  127.0 15.4 %all-to-all-start = ((bf16[16,8,1024]{2,0,1:T(8,128)(2,1)}), bf16[16,8,1024]{2,0,1:T(8,128)(2,1)S(1)}, u32[]{:S(2)}, u32[]{:S(2)}) async-start(bf16[16,8,1024]{2,0,1:T(8,128)(2,1)} %bitcast.51), calls=%async_computation | async-start | bytes 524288 | tf_op jit(solution)/shard_map/all_to_all | solution.py:403
  142.5 8.0 %scatter_custom_fusion = s32[2048]{0:T(1024)S(1)} fusion(s32[2048]{0:T(1024)S(1)} %compare_select_fusion.1, s32[2048]{0:T(1024)S(1)} %iota.7, s32[]{:T(128)} %constant.44.clone.1), kind=kCustom, calls=%fused_computation.96 | custom fusion | bytes 8196 | tf_op jit(solution)/shard_map/scatter | solution.py:352
  150.6 0.7 copy-done.4
  151.3 28.8 %plane_gather_5.1 = bf16[16,128,1024]{2,1,0:T(8,128)(2,1)} custom-call(bf16[128,1024]{1,0:T(8,128)(2,1)} %bitcast.58), custom_call_target="tpu_custom_call" | custom-call | tf_op jit(solution)/shard_map/plane_gather_5/pallas_call | solution.py:235
  180.0 5.0 %copy.18 = bf16[8,16,16,1024]{3,2,1,0:T(8,128)(2,1)} copy(bf16[8,16,16,1024]{3,2,0,1:T(8,128)(2,1)} %bitcast.53) | data formatting | bytes 8388608 | tf_op jit(solution)/shard_map/transpose | solution.py:408
  185.0 13.7 %gather_fusion = bf16[2048,1024]{1,0:T(8,128)(2,1)} fusion(bf16[2048,1024]{1,0:T(8,128)(2,1)} %bitcast.52, s32[2048]{0:T(1024)S(1)} %fusion.58), kind=kCustom, calls=%fused_computation | custom fusion | bytes 8396800 | tf_op jit(solution)/shard_map/jit(_take)/gather | solution.py:412
  198.7 3.1 multiply_reduce_fusion
  201.8 10.2 %all_to_all.25 = f32[8,1,2048]{2,1,0:T(1,128)S(1)} all-to-all(f32[8,1,2048]{2,1,0:T(1,128)S(1)} %broadcast_in_dim.42), channel_id=1, replica_groups=mesh['seq'=8,'tp_0'=4,'tp_1'=4] {'seq'}, dimensions={0} | all-to-all | bytes 131072 | tf_op jit(solution)/shard_map/all_to_all | solution.py:287
  212.0 0.1 reduce_sum.79
  212.1 22.3 %convolution_convert_fusion = bf16[2048,3696]{0,1:T(8,128)(2,1)} fusion(bf16[1024,3696]{0,1:T(8,128)(2,1)} %bitcast.60, f32[1024]{0:T(1024)S(1)} %copy-done.7, f32[2048]{0:T(1024)S(1)} %add_rsqrt_fusion, bf16[2048,1024]{1,0:T(8,128)(2,1)} %gather_fusion, pred[2048]{0:T(1024)(128)(4,1)S(1)} %compare_and_fusion), kind=kOutput, calls=%fused_computation.2 | convolution fusion | flops 15520202752 | bytes 26916864 | tf_op jit(solution)/shard_map/dot_general | solution.py:423
  234.4 0.0 reduce-scatter.4.cloned.1.call-update
  234.4 0.0 all-gather.2.cloned.1.call-start
  234.5 81.9 %reduce-scatter.4.cloned.1.call-done = bf16[256,3696]{0,1:T(8,128)(2,1)} async-done(((bf16[2048,3696]{0,1:T(8,128)(2,1)}), bf16[256,3696]{0,1:T(8,128)(2,1)}) %reduce-scatter.4.cloned.1.call-update) | async-done | bytes 1892368 | tf_op jit(solution)/shard_map/reduce_scatter | solution.py:422
  316.4 1.8 convert_element_type.77
  318.2 1.6 fusion.6
  319.8 0.0 all-gather.2.cloned.1.call-update
  319.8 0.0 reduce-scatter.6.cloned.1.call-start
  319.8 50.5 %all-gather.2.cloned.1.call-done = bf16[2048,1848]{0,1:T(8,128)(2,1)} async-done(((bf16[256,1848]{0,1:T(8,128)(2,1)}), bf16[2048,1848]{0,1:T(8,128)(2,1)}) %all-gather.2.cloned.1.call-update) | async-done | bytes 7569424 | tf_op jit(solution)/shard_map/all_gather | solution.py:432
  370.4 13.7 %convolution_convert_fusion.3 = bf16[2048,1024]{1,0:T(8,128)(2,1)} fusion(bf16[2048,1848]{0,1:T(8,128)(2,1)} %all-gather.2.cloned.1.call-done, bf16[1848,1024]{1,0:T(8,128)(2,1)} %param.23), kind=kOutput, calls=%fused_computation.14 | convolution fusion | flops 7753170944 | bytes 15548416 | tf_op jit(solution)/shard_map/dot_general | solution.py:431
  384.1 0.0 reduce-scatter.6.cloned.1.call-update
  384.1 0.0 reduce-scatter.8.cloned.1.call-start
  384.2 47.4 %reduce-scatter.6.cloned.1.call-done = bf16[512,1024]{1,0:T(8,128)(2,1)} async-done(((bf16[2048,1024]{1,0:T(8,128)(2,1)}), bf16[512,1024]{1,0:T(8,128)(2,1)}) %reduce-scatter.6.cloned.1.call-update) | async-done | bytes 1048592 | tf_op jit(solution)/shard_map/reduce_scatter | solution.py:320
  431.6 0.0 reduce-scatter.8.cloned.1.call-update
  431.7 5.3 %fusion.95 = f32[2048,1024]{1,0:T(8,128)} fusion(bf16[2048,1024]{1,0:T(8,128)(2,1)} %gather_fusion, pred[2048]{0:T(1024)(128)(4,1)S(1)} %compare_and_fusion), kind=kLoop, calls=%fused_computation.135 | loop fusion | flops 4194304 | bytes 12584960 | tf_op jit(solution)/shard_map/convert_element_type | solution.py:413
  437.0 19.2 %reduce-scatter.8.cloned.1.call-done = bf16[128,1024]{1,0:T(8,128)(2,1)} async-done(((bf16[512,1024]{1,0:T(8,128)(2,1)}), bf16[128,1024]{1,0:T(8,128)(2,1)}) %reduce-scatter.8.cloned.1.call-update) | async-done | bytes 262160 | tf_op jit(solution)/shard_map/reduce_scatter | solution.py:320
  456.2 1.9 add_convert_fusion
  (27 shorter events, 0.1 us)
Async XLA Ops:
  6.5 86.2 %copy-start = (bf16[5120,320]{0,1:T(8,128)(2,1)S(1)}, bf16[5120,320]{0,1:T(8,128)(2,1)}, u32[]{:S(2)}) copy-start(bf16[5120,320]{0,1:T(8,128)(2,1)} %param.19) | copy-start | bytes 9830404
  38.2 0.9 copy-start.8
  39.1 1.9 copy-start.3
  42.1 26.1 %copy-start.2 = (bf16[64,1280]{1,0:T(8,128)(2,1)S(1)}, bf16[64,1280]{1,0:T(8,128)(2,1)}, u32[]{:S(2)}) copy-start(bf16[64,1280]{1,0:T(8,128)(2,1)} %param.12) | copy-start | bytes 491524
  42.1 28.4 %copy-start.6 = (f32[1280]{0:T(1024)S(1)}, f32[1280]{0:T(1024)}, u32[]{:S(2)}) copy-start(f32[1280]{0:T(1024)} %param.18) | copy-start | bytes 15364
  103.9 38.6 %copy-start.5 = (s32[2048]{0:T(1024)S(1)}, s32[2048]{0:T(1024)}, u32[]{:S(2)}) copy-start(s32[2048]{0:T(1024)} %param.14) | copy-start | bytes 24580
  127.0 23.5 %all-to-all-start = ((bf16[16,8,1024]{2,0,1:T(8,128)(2,1)}), bf16[16,8,1024]{2,0,1:T(8,128)(2,1)S(1)}, u32[]{:S(2)}, u32[]{:S(2)}) async-start(bf16[16,8,1024]{2,0,1:T(8,128)(2,1)} %bitcast.51), calls=%async_computation | async-start | bytes 524288 | tf_op jit(solution)/shard_map/all_to_all | solution.py:403
  142.4 173.9 %reduce-scatter.4.cloned.1.call-start = ((), (), s32[]{:S(2)}) async-start(), calls=%async_computation.5 | async-start | bytes 17031168 | tf_op jit(solution)/shard_map/reduce_scatter | solution.py:422
  150.6 0.7 copy-start.4
  198.7 13.4 %copy-start.7 = (f32[1024]{0:T(1024)S(1)}, f32[1024]{0:T(1024)}, u32[]{:S(2)}) copy-start(f32[1024]{0:T(1024)} %param.21) | copy-start | bytes 12292
  234.4 135.9 %all-gather.2.cloned.1.call-start = ((), (), s32[]{:S(2)}) async-start(), calls=%async_computation.6 | async-start | bytes 8515584 | tf_op jit(solution)/shard_map/all_gather | solution.py:432
  319.8 111.8 %reduce-scatter.6.cloned.1.call-start = ((), (), s32[]{:S(2)}) async-start(), calls=%async_computation.7 | async-start | bytes 5242880 | tf_op jit(solution)/shard_map/reduce_scatter | solution.py:320
  384.1 72.0 %reduce-scatter.8.cloned.1.call-start = ((), (), s32[]{:S(2)}) async-start(), calls=%async_computation.8 | async-start | bytes 1310720 | tf_op jit(solution)/shard_map/reduce_scatter | solution.py:320
  431.7 26.4 %copy-start.1 = (bf16[5120,320]{0,1:T(8,128)(2,1)S(1)}, bf16[5120,320]{0,1:T(8,128)(2,1)}, u32[]{:S(2)}) copy-start(bf16[5120,320]{0,1:T(8,128)(2,1)} %param.19) | copy-start | bytes 9830404
Sparse Core Ops, SparseCore 0:
  234.5 81.7 reduce-scatter.3
  319.9 50.4 all-gather.1
  384.3 47.3 reduce-scatter.5
  433.9 22.2 reduce-scatter.7

commit v2 on v1

--- a/solution.py
+++ b/solution.py
@@ -7,6 +7,11 @@
 from jax.sharding import Mesh
 from jax.sharding import PartitionSpec as P
 
+D = 8192
+HD = 80
+TP = ("tp_0", "tp_1")
+SEQ_TP = ("seq", "tp_0", "tp_1")
+
 MESH_ID = pl.DeviceIdType.MESH
 AXES = ("tp_0", "tp_1")
 
@@ -32,14 +37,17 @@
     return [ring(axis, step) for axis in AXES for step in (1, 3)]
 
 
-def gather_plane(own, slot, half_cut, quarter_cut, send, recv, ready=None):
+def gather_plane(own, slot, half_cut, quarter_cut, send, recv, forward=None):
     here = [lax.axis_index(axis) for axis in AXES]
     sent = []
 
-    def place(half, first, second):
+    def index(half, first, second):
         offsets = (first, second) if half == 0 else (second, first)
         spots = [lax.rem(at + off, 4) for at, off in zip(here, offsets)]
-        return slot(spots[0] * 4 + spots[1])
+        return spots[0] * 4 + spots[1]
+
+    def place(half, first, second):
+        return slot(index(half, first, second))
 
     def source(half, first, second):
         return own if (first, second) == (0, 0) else place(half, first, second)
@@ -56,6 +64,8 @@
         at = half * 20 + phase * 4 + kind
         target = cut(place(half, first, second))
         remote(target, target, send.at[at], recv.at[at], ring(axis, 1)).wait_recv()
+        if forward is not None:
+            forward(at, lambda base: cut(base(index(half, first, second))))
 
     def axes(half):
         return (AXES[0], AXES[1]) if half == 0 else (AXES[1], AXES[0])
@@ -120,7 +130,7 @@
         copy.wait_send()
 
 
-def reduce_plane(term, quarter_cut, got, made, sums, send, recv, emit):
+def reduce_plane(term, got, made, sums, send, recv, emit):
     here = [lax.axis_index(axis) for axis in AXES]
     sent = []
 
@@ -130,7 +140,7 @@
     def part(half, first, second, which):
         offsets = (first, second) if half == 0 else (second, first)
         spots = [lax.rem(at + off, 4) for at, off in zip(here, offsets)]
-        return quarter_cut(term(spots[0] * 4 + spots[1]), 2 * half + which)
+        return term(spots[0] * 4 + spots[1], 2 * half + which)
 
     def phase_source(half, phase):
         if phase < 4:
@@ -258,7 +268,7 @@
         def emit(at, value):
             cut(out, at)[...] = value.astype(out.dtype)
 
-        reduce_plane(lambda t: terms_ref.at[t], cut, got, made, sums, send, recv, emit)
+        reduce_plane(lambda t, at: cut(terms_ref.at[t], at), got, made, sums, send, recv, emit)
 
     return pl.pallas_call(
         kernel,
@@ -275,50 +285,338 @@
         compiler_params=pltpu.CompilerParams(collective_id=collective_id, has_side_effects=True),
         name=f"plane_reduce_{collective_id}",
     )(terms)
-
-D = 8192
-HD = 80
-TP = ("tp_0", "tp_1")
-SEQ_TP = ("seq", "tp_0", "tp_1")
-
-
-def from_everyone(x, axis):
-    copies = jnp.broadcast_to(x, (lax.axis_size(axis), *x.shape))
-    return lax.all_to_all(copies, axis, split_axis=0, concat_axis=0, tiled=True)
-
-
-def laid_out(tiles, dim):
-    shape = list(tiles.shape[1:])
-    shape[dim] *= tiles.shape[0]
-    return jnp.moveaxis(tiles, 0, dim).reshape(shape)
-
-
-def gathered_copies(x, axis, dim):
-    tiles = from_everyone(x, axis)
-    return laid_out(tiles, dim)
-
-
-def cut_along(x, dim, devices):
-    before, after = (x.shape[:dim], x.shape[dim + 1 :])
-    return jnp.moveaxis(x.reshape(*before, devices, -1, *after), dim, 0)
-
-
-def sum_at_owner(x, axis, dim):
-    devices = lax.axis_size(axis)
-    tiles = lax.all_to_all(cut_along(x, dim, devices), axis, 0, 0, tiled=True)
-    return jnp.sum(tiles.astype(jnp.float32), axis=0)
-
-
-def over_copies(x, axis):
-    everything = from_everyone(x, axis)
-    return jnp.sum(everything, axis=0)
-
-
-def sum_by_axis(x, axes, dim):
-    if not axes:
-        return x
-    nearer = lax.psum_scatter(x, axes[0], scatter_dimension=dim, tiled=True)
-    return sum_by_axis(nearer, axes[1:], dim)
+WIDE = 2176
+PADDED = 1920
+
+
+def along_x(step):
+    seq = lax.axis_index("seq")
+    return {"seq": lax.rem(seq + 2 * step, 8)}
+
+
+def partner():
+    seq = lax.axis_index("seq")
+    return {"seq": seq + 1 - 2 * lax.rem(seq, 2)}
+
+
+def token_kernel(terms_ref, out, got, made, sums, vis, parcels, block, send, recv, xsend, xrecv, gsend, grecv, dsend, drecv):
+    greet(plane_neighbours() + [along_x(step) for step in (1, 2, 3)] + [partner()])
+    seq = lax.axis_index("seq")
+    x, core = seq // 2, lax.rem(seq, 2)
+    me = lax.axis_index("tp_0") * 4 + lax.axis_index("tp_1")
+
+    def emit(at, value):
+        parcels[at, :, :2048] = value.astype(jnp.bfloat16)
+
+    reduce_plane(lambda t, at: terms_ref.at[t, :, pl.ds(at * 2048, 2048)], got, made, sums, send, recv, emit)
+    squares = jnp.zeros((16, 1), jnp.float32)
+    for at in range(4):
+        values = parcels[at, :, :2048].astype(jnp.float32)
+        squares = squares + jnp.sum(values * values, axis=1, keepdims=True)
+    high = squares.astype(jnp.bfloat16).astype(jnp.float32)
+    low = squares - high
+    lane = lax.broadcasted_iota(jnp.int32, (16, 128), 1)
+    tail = jnp.where(lane == 0, high, jnp.where(lane == 1, low, 0.0)).astype(jnp.bfloat16)
+    for at in range(4):
+        parcels[at, :, 2048:] = tail
+    mine = pl.ds(pl.multiple_of(x * 16, 16), 16)
+    sent = []
+    for step in (2, 1, 3):
+        copy = remote(
+            parcels.at[lax.rem(x + step, 4)], block.at[mine, :], xsend.at[step], xrecv.at[step], along_x(step)
+        )
+        copy.start()
+        sent.append(copy)
+    block[mine, :] = parcels[x]
+    for step in (1, 3, 2):
+        rows = pl.ds(pl.multiple_of(lax.rem(x + 4 - step, 4) * 16, 16), 16)
+        landing = block.at[rows, :]
+        remote(landing, landing, xsend.at[step], xrecv.at[step], along_x(step)).wait_recv()
+    for copy in sent:
+        copy.wait_send()
+    forwarded = []
+    expected = []
+
+    def forward(at, view):
+        piece = view(lambda t: out.at[core, t])
+        copy = remote(piece, piece, dsend.at[at], drecv.at[at], partner())
+        copy.start()
+        forwarded.append(copy)
+        other = view(lambda t: out.at[1 - core, t])
+        expected.append(remote(other, other, dsend.at[at], drecv.at[at], partner()))
+
+    own_copy = remote(block, out.at[core, me], dsend.at[40], drecv.at[40], partner())
+    own_copy.start()
+    out[core, me] = block[...]
+    gather_plane(
+        block,
+        lambda t: out.at[core, t],
+        lambda ref, half: ref.at[pl.ds(half * 32, 32), :],
+        lambda ref, at: ref.at[pl.ds(at * 16, 16), :],
+        gsend,
+        grecv,
+        forward,
+    )
+    other = out.at[1 - core, me]
+    expected.append(remote(other, other, dsend.at[40], drecv.at[40], partner()))
+    own_copy.wait_send()
+    for copy in forwarded:
+        copy.wait_send()
+    for copy in expected:
+        copy.wait_recv()
+
+
+def all_tokens_of(terms, collective_id):
+    return pl.pallas_call(
+        token_kernel,
+        out_shape=jax.ShapeDtypeStruct((2, 16, 64, WIDE), jnp.bfloat16),
+        in_specs=[pl.BlockSpec(memory_space=pltpu.VMEM)],
+        out_specs=pl.BlockSpec(memory_space=pltpu.VMEM),
+        scratch_shapes=[
+            pltpu.VMEM((60, 16, 2048), jnp.bfloat16),
+            pltpu.VMEM((20, 16, 2048), jnp.bfloat16),
+            pltpu.VMEM((16, 16, 2048), jnp.bfloat16),
+            pltpu.VMEM((8, 128), jnp.float32),
+            pltpu.VMEM((4, 16, WIDE), jnp.bfloat16),
+            pltpu.VMEM((64, WIDE), jnp.bfloat16),
+            pltpu.SemaphoreType.DMA((60,)),
+            pltpu.SemaphoreType.DMA((60,)),
+            pltpu.SemaphoreType.DMA((4,)),
+            pltpu.SemaphoreType.DMA((4,)),
+            pltpu.SemaphoreType.DMA((40,)),
+            pltpu.SemaphoreType.DMA((40,)),
+            pltpu.SemaphoreType.DMA((41,)),
+            pltpu.SemaphoreType.DMA((41,)),
+        ],
+        compiler_params=pltpu.CompilerParams(
+            collective_id=collective_id, has_side_effects=True, vmem_limit_bytes=48 * 1024 * 1024
+        ),
+        name="all_tokens",
+    )(terms)
+
+
+def feed_forward_kernel(
+    tokens, gain, w_own, w_other, d_own, d_other, out,
+    weights, downs, rows, parts, came, hidden, products, got, made, sums, fin,
+    wsem, osem, psend, precv, hsend, hrecv, send, recv, fsend, frecv,
+):
+    seq = lax.axis_index("seq")
+    x, core = seq // 2, lax.rem(seq, 2)
+    me = lax.axis_index("tp_0") * 4 + lax.axis_index("tp_1")
+    real = w_own.shape[1]
+    weights[:, pl.ds(1840, 80), :] = jnp.zeros((2, 80, 2048), jnp.bfloat16)
+    downs[pl.ds(1840, 80), :] = jnp.zeros((80, 2048), jnp.bfloat16)
+    sides = ((w_own, d_own, core), (w_other, d_other, 1 - core))
+
+    def weight_copies(n):
+        size = 256 if n < 7 else real - 1792
+        return [
+            pltpu.make_async_copy(
+                w.at[:, pl.ds(n * 256, size), :],
+                weights.at[:, pl.ds(n * 256, size), pl.ds(pl.multiple_of(at * 1024, 1024), 1024)],
+                wsem.at[n, side],
+            )
+            for side, (w, _, at) in enumerate(sides)
+        ]
+
+    def down_copies():
+        return [
+            pltpu.make_async_copy(
+                d, downs.at[pl.ds(0, real), pl.ds(pl.multiple_of(at * 1024, 1024), 1024)], osem.at[side]
+            )
+            for side, (_, d, at) in enumerate(sides)
+        ]
+
+    for n in range(8):
+        for copy in weight_copies(n):
+            copy.start()
+    for copy in down_copies():
+        copy.start()
+
+    def owner(step):
+        return lax.rem(x + step, 4)
+
+    def multiply(step, first=False):
+        at = owner(step)
+        square = tokens[at, :, 2048:2049].astype(jnp.float32) + tokens[at, :, 2049:2050].astype(jnp.float32)
+        inverse = lax.rsqrt(square / D + 1e-06)
+        rows[...] = (tokens[at, :, :2048].astype(jnp.float32) * inverse * gain[...]).astype(jnp.bfloat16)
+
+        def piece(begin, size):
+            for half in range(2):
+                value = lax.dot_general(
+                    rows[...], weights[half, pl.ds(begin, size), :], (((1,), (1,)), ((), ())),
+                    preferred_element_type=jnp.float32,
+                )
+                parts[step, half, :, pl.ds(begin, size)] = value.astype(jnp.bfloat16)
+
+        if first:
+            for n in range(8):
+                for copy in weight_copies(n):
+                    copy.wait()
+                piece(n * 256, 256 if n < 7 else 128)
+        else:
+            @pl.loop(0, 7)
+            def _(n):
+                piece(pl.multiple_of(n * 256, 256), 256)
+
+            piece(1792, 128)
+
+    def cut(ref, sub):
+        return ref.at[:, pl.ds(sub * 64, 64), :]
+
+    sent = []
+
+    def pass_part(kind, index, src, step):
+        at = kind * 2 + index
+        copy = remote(src, came.at[at], psend.at[at], precv.at[at], along_x(step))
+        copy.start()
+        sent.append(copy)
+
+    def part_landed(kind, index):
+        at = kind * 2 + index
+        remote(came.at[at], came.at[at], psend.at[at], precv.at[at], along_x(1)).wait_recv()
+        return came.at[at]
+
+    multiply(2, True)
+    greet(plane_neighbours() + [along_x(step) for step in (1, 3)] + [partner()])
+    for index in range(2):
+        pass_part(0, index, cut(parts.at[2], index), 1)
+        pass_part(3, index, cut(parts.at[2], 2 + index), 3)
+    multiply(1)
+    for index in range(2):
+        pass_part(1, index, cut(parts.at[1], 2 + index), 1)
+    multiply(3)
+    for index in range(2):
+        pass_part(4, index, cut(parts.at[3], index), 3)
+    for index in range(2):
+        for kind, step, sub, way in ((0, 1, index, 1), (3, 3, 2 + index, 3)):
+            arrived = part_landed(kind, index)
+            target = cut(parts.at[step], sub)
+            target[...] = (target[...].astype(jnp.float32) + arrived[...].astype(jnp.float32)).astype(jnp.bfloat16)
+            pass_part(kind + 2, index, target, way)
+    multiply(0)
+
+    def hidden_piece(step, sub):
+        return hidden.at[owner(step), pl.ds(sub * 64, 64), :]
+
+    def pass_hidden(at, piece, step):
+        copy = remote(piece, piece, hsend.at[at], hrecv.at[at], along_x(step))
+        copy.start()
+        sent.append(copy)
+
+    def hidden_landed(at, piece):
+        remote(piece, piece, hsend.at[at], hrecv.at[at], along_x(1)).wait_recv()
+
+    for index in range(2):
+        for sub, near, far in ((index, 4, 2), (2 + index, 1, 5)):
+            one = part_landed(near, index)
+            two = part_landed(far, index)
+            own = cut(parts.at[0], sub)
+            gate, up = [
+                own[half].astype(jnp.float32) + one[half].astype(jnp.float32) + two[half].astype(jnp.float32)
+                for half in range(2)
+            ]
+            piece = hidden_piece(0, sub)
+            piece[...] = (gate / (1.0 + jnp.exp(-gate)) * up).astype(jnp.bfloat16)
+            pass_hidden(sub, piece, 1)
+            pass_hidden(4 + sub, piece, 3)
+    for copy in down_copies():
+        copy.wait()
+
+    def project(step):
+        at = owner(step)
+
+        @pl.loop(0, 8)
+        def _(n):
+            begin = pl.multiple_of(n * 256, 256)
+            value = jnp.dot(hidden[at], downs[:, pl.ds(begin, 256)], preferred_element_type=jnp.float32)
+            products[at, :, pl.ds(begin, 256)] = value.astype(jnp.bfloat16)
+
+    def relay(index):
+        hidden_landed(index, hidden_piece(3, index))
+        pass_hidden(8 + index, hidden_piece(3, index), 1)
+        hidden_landed(4 + 2 + index, hidden_piece(1, 2 + index))
+        pass_hidden(10 + index, hidden_piece(1, 2 + index), 3)
+
+    project(0)
+    relay(0)
+    relay(1)
+    for index in range(2):
+        hidden_landed(2 + index, hidden_piece(3, 2 + index))
+    project(3)
+    for index in range(2):
+        hidden_landed(4 + index, hidden_piece(1, index))
+    project(1)
+    for index in range(2):
+        hidden_landed(8 + index, hidden_piece(2, index))
+        hidden_landed(10 + index, hidden_piece(2, 2 + index))
+    project(2)
+
+    turns = (0, 3, 1, 2)
+    strip = pl.ds(pl.multiple_of(me * 16, 16), 16)
+
+    def term(t, at):
+        return products.at[owner(turns[at]), pl.ds(pl.multiple_of(t * 16, 16), 16), :]
+
+    def emit(at, value):
+        q = owner(turns[at])
+        total = (value + tokens[q, strip, :2048].astype(jnp.float32)).astype(jnp.bfloat16)
+        target = pl.ds(pl.multiple_of(q * 16, 16), 16)
+        fin[0, target, :] = total[:, :1024]
+        fin[1, target, :] = total[:, 1024:]
+
+    reduce_plane(term, got, made, sums, send, recv, emit)
+    mine = pl.ds(pl.multiple_of(core * 64, 64), 64)
+    theirs = pl.ds(pl.multiple_of((1 - core) * 64, 64), 64)
+    swap = remote(fin.at[1 - core], out.at[mine, :], fsend, frecv, partner())
+    swap.start()
+    out[mine, :] = fin[core]
+    swap.wait_send()
+    landing = out.at[theirs, :]
+    remote(landing, landing, fsend, frecv, partner()).wait_recv()
+    for copy in sent:
+        copy.wait_send()
+
+
+def feed_forward(tokens, gain, w_own, w_other, d_own, d_other, collective_id):
+    anywhere = pl.BlockSpec(memory_space=pl.ANY)
+    vmem = pl.BlockSpec(memory_space=pltpu.VMEM)
+    dma = pltpu.SemaphoreType.DMA
+    bf16 = jnp.bfloat16
+    return pl.pallas_call(
+        feed_forward_kernel,
+        out_shape=jax.ShapeDtypeStruct((128, 1024), bf16),
+        in_specs=[vmem, vmem, anywhere, anywhere, anywhere, anywhere],
+        out_specs=vmem,
+        scratch_shapes=[
+            pltpu.VMEM((2, PADDED, 2048), bf16),
+            pltpu.VMEM((PADDED, 2048), bf16),
+            pltpu.VMEM((256, 2048), bf16),
+            pltpu.VMEM((4, 2, 256, PADDED), bf16),
+            pltpu.VMEM((12, 2, 64, PADDED), bf16),
+            pltpu.VMEM((4, 256, PADDED), bf16),
+            pltpu.VMEM((4, 256, 2048), bf16),
+            pltpu.VMEM((60, 16, 2048), bf16),
+            pltpu.VMEM((20, 16, 2048), bf16),
+            pltpu.VMEM((16, 16, 2048), bf16),
+            pltpu.VMEM((2, 64, 1024), bf16),
+            dma((8, 2)),
+            dma((2,)),
+            dma((12,)),
+            dma((12,)),
+            dma((12,)),
+            dma((12,)),
+            dma((60,)),
+            dma((60,)),
+            dma,
+            dma,
+        ],
+        compiler_params=pltpu.CompilerParams(
+            collective_id=collective_id, has_side_effects=True, vmem_limit_bytes=67043328
+        ),
+        name="feed_forward",
+    )(tokens, gain, w_own, w_other, d_own, d_other)
 
 
 def layer_norm(values, gain):
@@ -347,9 +645,13 @@
     return output.astype(jnp.bfloat16)
 
 
-def slot_sources(positions):
-    count = positions.shape[0]
-    return jnp.zeros((count,), jnp.int32).at[positions].set(jnp.arange(count, dtype=jnp.int32))
+def sources(positions, core):
+    row = jnp.arange(1024, dtype=jnp.int32)
+    slot = (row // 16 % 16) * 128 + core * 64 + (row // 256) * 16 + row % 16
+    index = jnp.arange(positions.shape[0], dtype=jnp.int32)
+    found = jnp.sum(jnp.where(positions[None, :] == slot[:, None], index[None, :], 0), axis=1)
+    group, within = found // 256, found % 256
+    return (group % 2) * 1024 + (within // 16) * 64 + (group // 2) * 16 + within % 16
 
 
 def local(
@@ -399,43 +701,20 @@
     ).astype(jnp.bfloat16)
     picked = expanded
     shares = jnp.dot(picked, merger_w2, preferred_element_type=jnp.float32).astype(jnp.bfloat16)
-    vis_rows = plane_reduce(shares.reshape(tp_size, own_tokens, D), 4, False, jnp.bfloat16)
-    blocks = lax.all_to_all(vis_rows, "seq", split_axis=1, concat_axis=0, tiled=True)
-    gathered = plane_gather(blocks, 5, True)
-    col_width = gathered.shape[2]
-    all_tokens = (
-        gathered.reshape(tp_size, seq_size, own_tokens, col_width)
-        .transpose(1, 0, 2, 3)
-        .reshape(tp_size * seq_size * own_tokens, col_width)
+    everyone = all_tokens_of(shares.reshape(tp_size, own_tokens, D), 4).reshape(-1, WIDE)
+    core = lax.rem(lax.axis_index("seq"), 2)
+    own_tokens_of_core = jnp.take(everyone, sources(positions, core), axis=0).reshape(4, 256, WIDE)
+    swap = [(i, i ^ 1) for i in range(seq_size)]
+    gate_up_rows = jnp.transpose(gate_up_weight, (1, 2, 0))
+    other_rows = lax.ppermute(gate_up_rows, "seq", swap)
+    other_down = lax.ppermute(down_weight, "seq", swap)
+    other_gain = lax.ppermute(norm_gain, "seq", swap)
+    gain = jnp.where(
+        core == 0, jnp.concatenate([norm_gain, other_gain]), jnp.concatenate([other_gain, norm_gain])
     )
-    seq_rows = all_tokens.shape[0]
-    seq_tokens = jnp.take(all_tokens, slot_sources(positions), axis=0)
-    token_values = seq_tokens.astype(jnp.float32)
-    row_squares = over_copies(jnp.sum(token_values * token_values, axis=1), "seq")
-    inverse_rms = lax.rsqrt(row_squares / D + 1e-06)
-    normed = (token_values * inverse_rms[:, None] * norm_gain).astype(jnp.bfloat16)
-    slice_width = seq_tokens.shape[1]
-    hidden_width = gate_up_weight.shape[2]
-    weight_flat = gate_up_weight.reshape(slice_width, 2 * hidden_width)
-    out_rows = seq_rows // tp_size
-    picked = normed
-    gate_up = lax.psum_scatter(
-        jnp.dot(picked, weight_flat, preferred_element_type=jnp.float32).astype(jnp.bfloat16),
-        "seq",
-        scatter_dimension=0,
-        tiled=True,
-    ).astype(jnp.float32)
-    hidden = (jax.nn.silu(gate_up[:, :hidden_width]) * gate_up[:, hidden_width:]).astype(
-        jnp.bfloat16
+    return feed_forward(
+        own_tokens_of_core, gain[None], gate_up_rows, other_rows, down_weight, other_down, 5
     )
-    terms = jnp.dot(
-        lax.all_gather(hidden, "seq", axis=0, tiled=True),
-        down_weight,
-        preferred_element_type=jnp.float32,
-    )
-    down_sum = sum_by_axis(terms.astype(jnp.bfloat16), TP, 0).astype(jnp.float32)
-    residual = lax.dynamic_slice_in_dim(token_values, lax.axis_index(TP) * out_rows, out_rows, 0)
-    return (residual + down_sum).astype(jnp.bfloat16)
 
 
 def solution(mesh):

time: 466 us -> 336 us (0.72)
  waiting for transfers between devices: 199 us -> 0.01 us
  Pallas kernels: 113 us -> 275 us
  matrix products: 56.7 us -> 21.5 us
  starting transfers between devices: 15.5 us -> 1.89 us
  between operations: 13.4 us -> 0.23 us
  local copies, waits for them, and re-layouts: 32.7 us -> 20.4 us
  blocking collectives: 10.2 us -> 0 us
  other arithmetic: 23.8 us -> 16.1 us
    pallas_call x0 -> x2, Pallas kernels: none -> 213 us  [the longest x1 140 us: feed_forward(): pl.pallas_call(feed_forward_kernel, out_shape=jax.ShapeDtypeStruct((128,...]
    reduce_scatter x3 -> x0, waiting for transfers between devices: 149 us -> none  [the longest x1 81.9 us: local(): lax.psum_scatter(jnp.dot(picked, weight_flat, preferred_element_type=jnp....]
    all_gather x1 -> x0, waiting for transfers between devices: 50.5 us -> none  [local(): lax.all_gather(hidden, 'seq', axis=0, tiled=True)]
    dot_general x2 -> x0, matrix products: 36.1 us -> none  [the longest x1 22.3 us: local(): jnp.dot(picked, weight_flat, preferred_element_type=jnp.float32)]
    pallas_call x3 -> x2, Pallas kernels: 71.5 us -> 41.9 us  [plane_gather(): pl.pallas_call(kernel, out_shape=jax.ShapeDtypeStruct((16, rows, cols), b...]
    pallas_call x2 -> x1, Pallas kernels: 41.6 us -> 20.4 us  [plane_reduce(): pl.pallas_call(kernel, out_shape=jax.ShapeDtypeStruct((rows, cols), out_d...]
    all_to_all x1 -> x0, starting transfers between devices: 15.4 us -> none  [local(): lax.all_to_all(vis_rows, 'seq', split_axis=1, concat_axis=0, tiled=True)]
    convert_element_type x4 -> x0, other arithmetic: 10.6 us -> none  [the longest x1 5.31 us: local(): token_values = seq_tokens.astype(jnp.float32)]
  transfers between devices with their start and end apart: 5 -> 3, of which waited for: 4 -> 0; matrix products, arithmetic and copies ran while one was open for 3% -> 16% of each run, Pallas kernels for 0% -> 40%
where the time goes in v2:
time: 336 us; the launch traced here: 335 us
  Pallas kernels  275 us (82%)
  matrix products  21.5 us (6%)
  local copies, waits for them, and re-layouts  20.4 us (6%)
  other arithmetic  16.1 us (5%)
    pallas_call x1, Pallas kernels, feed_forward(): pl.pallas_call(feed_forward_kernel, out_shape=jax.ShapeDtypeStruct((128,...  140 us
    pallas_call x1, Pallas kernels, all_tokens_of(): pl.pallas_call(token_kernel, out_shape=jax.ShapeDtypeStruct((2, 16, 64, W...  72.2 us
    pallas_call x2, Pallas kernels, plane_gather(): pl.pallas_call(kernel, out_shape=jax.ShapeDtypeStruct((16, rows, cols), b...  41.9 us
    pallas_call x1, Pallas kernels, plane_reduce(): pl.pallas_call(kernel, out_shape=jax.ShapeDtypeStruct((rows, cols), out_d...  20.4 us
    gather x1, local copies, waits for them, and re-layouts, local(): jnp.take(everyone, sources(positions, core), axis=0).reshape(4, 256, WIDE)  13.8 us
    dot_general x1, matrix products, local(): jnp.dot(picked, merger_w2, preferred_element_type=jnp.float32)  12.1 us
  transfers between devices with their start and end apart: 3, of which 0 were waited for; matrix products, arithmetic and copies ran while one was open for 16% of the time, Pallas kernels for 40%

profile of v2, /device:TPU:1, one launch (start us, length us, event | category | flops | bytes accessed | tf_op | source)
XLA Modules:
  0.0 335.2 jit_solution(8125812052236897229)
XLA Ops:
  0.0 1.4 collective-permute-start
  1.4 0.0 collective-permute-start.1
  1.4 0.5 collective-permute-start.2
  1.9 1.0 convert_reduce_fusion
  2.9 1.1 fusion.7
  4.1 1.7 fusion.9.own
  5.8 23.7 %plane_gather_1.1 = bf16[16,64,1280]{2,1,0:T(8,128)(2,1)} custom-call(bf16[64,1280]{1,0:T(8,128)(2,1)} %fusion.9.own), custom_call_target="tpu_custom_call" | custom-call | tf_op jit(solution)/shard_map/plane_gather_1/pallas_call | solution.py:245
  29.5 0.8 reduce-window.8
  30.3 0.1 fusion.53
  30.4 2.7 convolution_convert_fusion.2
  33.1 0.0 copy-start.5
  33.2 0.9 fusion.1
  34.0 0.0 copy-start.2
  34.0 1.9 copy-done.2
  36.0 1.0 fusion
  37.0 0.0 copy-done.5
  37.0 0.0 copy-start.1
  37.0 0.0 copy-start.3
  37.0 5.9 %convolution_convert_fusion.1 = bf16[1024,1280]{1,0:T(8,128)(2,1)} fusion(bf16[80,1280]{1,0:T(8,128)(2,1)S(1)} %copy-done.5, f32[1024,1024]{0,1:T(8,128)} %copy-done.2, f32[1024]{0:T(1024)S(1)} %fusion, f32[1024]{0:T(1024)S(1)} %get-tuple-element.5, s32[1024]{0:T(1024)S(1)} %fusion.53, bf16[1024,3,1,80]{0,3,1,2:T(8,128)(2,1)S(1)} %bitcast.59), kind=kOutput, calls=%fused_computation.7 | convolution fusion | flops 385171456 | bytes 7200768 | tf_op jit(solution)/shard_map/dot_general | solution.py:689
  42.9 20.4 %plane_reduce_2.1 = f32[64,1280]{1,0:T(8,128)} custom-call(bf16[16,64,1280]{2,1,0:T(8,128)(2,1)} %bitcast.50), custom_call_target="tpu_custom_call" | custom-call | tf_op jit(solution)/shard_map/plane_reduce_2/pallas_call | solution.py:273
  63.3 0.0 copy-done.1
  63.3 1.1 fusion.52
  64.5 1.2 multiply_reduce_fusion
  65.7 0.0 copy-done.3
  65.7 1.1 multiply_convert_fusion
  66.8 0.8 reshape.459.own
  67.5 18.3 %plane_gather_3.1 = bf16[16,16,5120]{2,1,0:T(8,128)(2,1)} custom-call(bf16[16,5120]{1,0:T(8,128)(2,1)} %reshape.459.own), custom_call_target="tpu_custom_call" | custom-call | tf_op jit(solution)/shard_map/plane_gather_3/pallas_call | solution.py:245
  85.8 12.1 %convolution_convert_fusion = bf16[256,8192]{1,0:T(8,128)(2,1)} fusion(bf16[320,8192]{1,0:T(8,128)(2,1)} %param.20, bf16[256,5120]{1,0:T(8,128)(2,1)} %bitcast.51, bf16[5120,320]{0,1:T(8,128)(2,1)} %param.19), kind=kOutput, calls=%fused_computation.1 | convolution fusion | flops 2188460032 | bytes 15335424 | tf_op jit(solution)/shard_map/dot_general | solution.py:703
  97.9 0.0 copy-start
  97.9 2.2 copy-done
  100.1 0.0 copy-start.6
  100.1 72.2 %all_tokens.1 = bf16[2,16,64,2176]{3,2,1,0:T(8,128)(2,1)} custom-call(bf16[16,16,8192]{2,1,0:T(8,128)(2,1)S(1)} %bitcast.44), custom_call_target="tpu_custom_call" | custom-call | tf_op jit(solution)/shard_map/all_tokens/pallas_call | solution.py:370
  172.3 0.0 copy-done.6
  172.3 1.3 select_reduce_fusion
  173.6 0.1 compare_select_fusion
  173.7 13.8 %gather_fusion = bf16[1024,2176]{1,0:T(8,128)(2,1)} fusion(bf16[2048,2176]{1,0:T(8,128)(2,1)} %bitcast.45, s32[1024]{0:T(1024)S(1)} %broadcast_clamp_fusion), kind=kCustom, calls=%fused_computation | custom fusion | bytes 8916992 | tf_op jit(solution)/shard_map/jit(_take)/gather | solution.py:706
  187.5 0.0 copy-start.4
  187.5 4.8 %broadcast_select_fusion.tokens = bf16[4,256,2176]{2,1,0:T(8,128)(2,1)} fusion(bf16[4,256,2176]{2,1,0:T(8,128)(2,1)} %bitcast.46, pred[4,256]{1,0:T(4,128)(4,1)S(1)} %compare_and_fusion), kind=kLoop, calls=%fused_computation.3 | loop fusion | flops 2228224 | bytes 8913920 | tf_op jit(solution)/shard_map/jit(_take)/select_n | solution.py:706
  192.4 0.0 collective-permute-done
  192.4 0.0 copy-done.4
  192.4 0.6 broadcast_select_fusion.1.gain
  193.0 0.0 collective-permute-done.2.d_other
  193.0 0.0 collective-permute-done.1.w_other
  193.0 140.5 %feed_forward.1 = bf16[128,1024]{1,0:T(8,128)(2,1)} custom-call(bf16[4,256,2176]{2,1,0:T(8,128)(2,1)} %broadcast_select_fusion.tokens, f32[1,2048]{1,0:T(1,128)} %broadcast_select_fusion.1.gain, bf16[2,1848,1024]{2,1,0:T(8,128)(2,1)} %bitcast.48, bf16[2,1848,1024]{2,1,0:T(8,128)(2,1)} %collective-permute-done.1.w_other, bf16[1848,1024]{1,0:T(8,128)(2,1)} %d_own.1, ...), custom_call_target="tpu_custom_call" | custom-call | tf_op jit(solution)/shard_map/feed_forward/pallas_call | solution.py:587
  333.5 1.7 copy.14
  (9 shorter events, 0.1 us)
Async XLA Ops:
  0.0 192.4 %collective-permute-start = (f32[1024]{0:T(1024)}, f32[1024]{0:T(1024)S(1)}, u32[]{:S(2)}, u32[]{:S(2)}) collective-permute-start(f32[1024]{0:T(1024)} %param.21), channel_id=1, source_target_pairs={{0,16},{16,0},{32,48},{48,32},{64,80},{80,64},{96,112},{112,96},{1... | collective-permute-start | bytes 12296 | tf_op jit(solution)/shard_map/ppermute | solution.py:711
  1.4 191.6 %collective-permute-start.1 = (bf16[2,1848,1024]{2,1,0:T(8,128)(2,1)}, bf16[2,1848,1024]{2,1,0:T(8,128)(2,1)}, u32[]{:S(2)}, u32[]{:S(2)}) collective-permute-start(bf16[2,1848,1024]{2,1,0:T(8,128)(2,1)} %bitcast.47), channel_id=1, source_target_pairs={{0,16},{16,0},{32,48},{48,32},{64,80},{80,64},{96,112},{112,96},{1... | collective-permute-start | bytes 22708232 | tf_op jit(solution)/shard_map/ppermute | solution.py:709
  1.4 191.6 %collective-permute-start.2 = (bf16[1848,1024]{1,0:T(8,128)(2,1)}, bf16[1848,1024]{1,0:T(8,128)(2,1)}, u32[]{:S(2)}, u32[]{:S(2)}) collective-permute-start(bf16[1848,1024]{1,0:T(8,128)(2,1)} %d_own.1), channel_id=1, source_target_pairs={{0,16},{16,0},{32,48},{48,32},{64,80},{80,64},{96,112},{112,96},{1... | collective-permute-start | bytes 11354120 | tf_op jit(solution)/shard_map/ppermute | solution.py:710
  33.1 3.8 %copy-start.5 = (bf16[80,1280]{1,0:T(8,128)(2,1)S(1)}, bf16[80,1280]{1,0:T(8,128)(2,1)}, u32[]{:S(2)}) copy-start(bf16[80,1280]{1,0:T(8,128)(2,1)} %param.17) | copy-start | bytes 614404
  34.0 1.9 copy-start.2
  37.0 26.3 %copy-start.1 = (bf16[64,1280]{1,0:T(8,128)(2,1)S(1)}, bf16[64,1280]{1,0:T(8,128)(2,1)}, u32[]{:S(2)}) copy-start(bf16[64,1280]{1,0:T(8,128)(2,1)} %param.12) | copy-start | bytes 491524
  37.0 28.7 %copy-start.3 = (f32[1280]{0:T(1024)S(1)}, f32[1280]{0:T(1024)}, u32[]{:S(2)}) copy-start(f32[1280]{0:T(1024)} %param.18) | copy-start | bytes 15364
  97.9 2.2 copy-start
  100.1 72.2 %copy-start.6 = (s32[2048]{0:T(1024)S(1)}, s32[2048]{0:T(1024)}, u32[]{:S(2)}) copy-start(s32[2048]{0:T(1024)} %param.14) | copy-start | bytes 24580
  187.5 4.9 %copy-start.4 = (f32[1024]{0:T(1024)S(1)}, f32[1024]{0:T(1024)}, u32[]{:S(2)}) copy-start(f32[1024]{0:T(1024)} %param.21) | copy-start | bytes 12292
